TPU v7x, 256 devices: a whole 4x4x8 slice. The times are simulated.
256 devices in a mesh: fsdp: 32 (over z_hi, x, core), tp: 8 (over y, z_lo).
Axes of the slice: x: 4, y: 4, z: 8 (z_hi: 4, z_lo: 2; z = z_hi * 2 + z_lo), core: 2. Of those that a mesh axis runs over, the one named last changes fastest.
Arguments:
- hidden: bfloat16 [8192, 8192], P('fsdp'), may hold values from -6 to 6
- norm_gain: float32 [8192], replicated, may hold values from 0.6 to 6, as said below
- w_query: bfloat16 [8192, 4096], P('fsdp', 'tp'), may hold values from -0.09375 to 0.09375
- w_key: bfloat16 [8192, 512], P('fsdp'), may hold values from -0.09375 to 0.09375
- w_value: bfloat16 [8192, 512], P('fsdp'), may hold values from -0.0625 to 0.0625
- bias_query: bfloat16 [4096], P('tp'), may hold values from -3 to 3
- bias_key: bfloat16 [512], replicated, may hold values from -3 to 3
- bias_value: bfloat16 [512], replicated, may hold values from -3 to 3
- w_out: bfloat16 [4096, 8192], P('tp', 'fsdp'), may hold values from -0.09375 to 0.09375
- seq_lengths: int32 [4], replicated, may hold values from 1 to 6144, 8192 in all
Outputs:
- hidden_out: float32 [8192, 8192], P(('fsdp', 'tp'))
Inputs may be any that keep to these rules, and one draw needn't show every extreme that they name: `seq_lengths`: 4 sequences packed in order; the lengths sum to 8192 and the longest has exactly 6144 tokens. `norm_gain`: positive gains.
All inputs are finite; a program needn't handle non-finite values.
Results may differ from a plain program's by a relative error of at most 0.014.
The roundings to bfloat16 on the way count: a program that leaves them out, or rounds other values in their place, can miss the bound.
Values may be sent and summed in bfloat16 or wider, within the bound.
No kernel may reach another device: no remote copies, remote signals or barrier semaphores. Data moves between devices by JAX's collectives and lax.ppermute only.
A program may use at most 128 MiB of HBM per device.

v0:
```python
import math
import jax
import jax.numpy as jnp
from jax import lax
from jax.sharding import Mesh
from jax.sharding import PartitionSpec as P

HEAD = 128
QHEADS = 32
KVHEADS = 4
TP = ("tp_0", "tp_1")
FSDP_TP = ("fsdp", "tp_0", "tp_1")
ROPE_BASE = 1000000.0
EPSILON = 1e-06
FLOOR = -1e30


def side_by_side(arrays, axis, dim, along):
    widths = [a.shape[along] for a in arrays]
    both = jnp.concatenate(arrays, axis=along)
    filled = lax.all_gather(both, axis, axis=dim, tiled=True)
    return tuple(jnp.split(filled, [sum(widths[:k]) for k in range(1, len(widths))], axis=along))


def scatter_axes(array, axes, dim):
    for axis in axes:
        array = lax.psum_scatter(array, axis, scatter_dimension=dim, tiled=True)
    return array


def token_layout(seq_lengths, token_index):
    seq_ends = jnp.cumsum(seq_lengths)
    seq_starts = seq_ends - seq_lengths
    member = (token_index[:, None] >= seq_ends[None, :]).astype(jnp.int32)
    segment = jnp.sum(member, axis=1)
    one_hot = segment[:, None] == jnp.arange(seq_lengths.shape[0], dtype=jnp.int32)[None, :]
    seq_begin = jnp.sum(jnp.where(one_hot, seq_starts[None, :], 0), axis=1)
    return (segment, token_index - seq_begin)


def rotary(vectors, position):
    half_size = vectors.shape[-1] // 2
    frequency = jnp.exp(
        jnp.arange(half_size, dtype=jnp.float32) * (-2.0 * math.log(ROPE_BASE) / vectors.shape[-1])
    )
    angle = position.astype(jnp.float32)[:, None] * frequency[None, :]
    cos_table = jnp.concatenate([jnp.cos(angle), jnp.cos(angle)], axis=1)[:, None, :]
    sin_table = jnp.concatenate([jnp.sin(angle), jnp.sin(angle)], axis=1)[:, None, :]
    turned = jnp.concatenate([-vectors[..., half_size:], vectors[..., :half_size]], axis=-1)
    return vectors * cos_table + turned * sin_table


def shards(
    hidden, norm_gain, w_query, w_key, w_value, bias_query, bias_key, bias_value, w_out, seq_lengths
):
    tok_rows = hidden.shape[0]
    first_row = lax.axis_index("fsdp") * tok_rows
    local_index = first_row + jnp.arange(tok_rows, dtype=jnp.int32)
    segment, position = token_layout(seq_lengths, local_index)
    widened = hidden.astype(jnp.float32)
    scale = lax.rsqrt(jnp.mean(widened * widened, axis=1, keepdims=True) + EPSILON)
    normed = (widened * scale * norm_gain[None, :]).astype(jnp.bfloat16)
    query_cols = w_query.shape[1]
    local_heads = query_cols // HEAD
    group_size = QHEADS // KVHEADS
    local_kv = max(local_heads // group_size, 1)
    first_kv = lax.axis_index(TP) * local_heads // group_size
    key_cols = local_kv * HEAD
    key_part = lax.dynamic_slice_in_dim(w_key, first_kv * HEAD, key_cols, 1)
    value_part = lax.dynamic_slice_in_dim(w_value, first_kv * HEAD, key_cols, 1)
    key_bias = lax.dynamic_slice_in_dim(bias_key, first_kv * HEAD, key_cols, 0)
    value_bias = lax.dynamic_slice_in_dim(bias_value, first_kv * HEAD, key_cols, 0)
    pieces = side_by_side((w_query, key_part, value_part), "fsdp", 0, 1)
    query, keys, values = tuple(
        (jnp.dot(normed, piece, preferred_element_type=jnp.float32) for piece in pieces)
    )
    query = rotary(
        (query + bias_query.astype(jnp.float32)[None, :]).reshape(tok_rows, -1, HEAD), position
    ).astype(jnp.bfloat16)
    keys = rotary(
        (keys + key_bias.astype(jnp.float32)[None, :]).reshape(tok_rows, -1, HEAD), position
    ).astype(jnp.bfloat16)
    values = (values + value_bias.astype(jnp.float32)[None, :]).astype(jnp.bfloat16)
    keys = keys.reshape(tok_rows, key_cols)
    per_kv = local_heads // local_kv
    query_grid = query.reshape(tok_rows, local_kv, per_kv, HEAD)
    start_state = (
        jnp.full((local_kv, per_kv, tok_rows), FLOOR, jnp.float32),
        jnp.zeros((local_kv, per_kv, tok_rows), jnp.float32),
        jnp.zeros((local_kv, per_kv, tok_rows, HEAD), jnp.float32),
    )
    key_piece, value_piece = side_by_side((keys, values), "fsdp", 0, 1)
    piece_rows = key_piece.shape[0]
    shard_count = max(piece_rows // tok_rows, 1)
    per_block = 1
    for divisor in range(1, 9):
        if shard_count % divisor == 0:
            per_block = divisor
    block_rows = min(per_block * tok_rows, piece_rows)
    block_count = piece_rows // block_rows

    def fold_block(block_number, carried):
        running_max, total, accumulated = carried
        offset = block_number * block_rows
        key_block = lax.dynamic_slice_in_dim(key_piece, offset, block_rows, 0).reshape(
            block_rows, local_kv, HEAD
        )
        value_block = lax.dynamic_slice_in_dim(value_piece, offset, block_rows, 0).reshape(
            block_rows, local_kv, HEAD
        )
        key_index = offset + jnp.arange(block_rows, dtype=jnp.int32)
        key_segment, unused = token_layout(seq_lengths, key_index)
        scores = jnp.einsum(
            "qkgd,nkd->kgqn", query_grid, key_block, preferred_element_type=jnp.float32
        ) * HEAD ** (-0.5)
        allowed = (
            (segment[:, None] == key_segment[None, :])
            & (local_index[:, None] >= key_index[None, :])
        )[None, None]
        scores = jnp.where(allowed, scores, FLOOR)
        new_max = jnp.maximum(running_max, jnp.max(scores, axis=3))
        weights = jnp.where(allowed, jnp.exp(scores - new_max[..., None]), 0.0)
        factor = jnp.exp(running_max - new_max)
        total = total * factor + jnp.sum(weights, axis=3)
        update = jnp.einsum(
            "kgqn,nkd->kgqd",
            weights.astype(jnp.bfloat16),
            value_block,
            preferred_element_type=jnp.float32,
        )
        accumulated = accumulated * factor[..., None] + update
        return (new_max, total, accumulated)

    final_state = lax.fori_loop(0, block_count, fold_block, start_state)
    mixed = final_state[2] / final_state[1][..., None]
    attended = jnp.transpose(mixed, (2, 0, 1, 3)).reshape(tok_rows, query_cols).astype(jnp.bfloat16)
    share_rows = tok_rows // lax.axis_size(TP)
    own_rows = lax.dynamic_slice_in_dim(
        hidden, lax.axis_index(TP) * share_rows, share_rows, 0
    ).astype(jnp.float32)
    terms = jnp.dot(
        attended,
        lax.all_gather(w_out, "fsdp", axis=1, tiled=True),
        preferred_element_type=jnp.float32,
    )
    summed = scatter_axes(terms.astype(jnp.bfloat16), TP, 0).astype(jnp.float32)
    return own_rows + summed


def solution(mesh):
    split = Mesh(mesh.devices.reshape(mesh.shape["fsdp"], 4, 2), ("fsdp", "tp_0", "tp_1"))
    return jax.shard_map(
        shards,
        mesh=split,
        in_specs=(
            P("fsdp", None),
            P(),
            P("fsdp", TP),
            P("fsdp", None),
            P("fsdp", None),
            P(TP),
            P(),
            P(),
            P(TP, "fsdp"),
            P(),
        ),
        out_specs=P(FSDP_TP, None),
        check_vma=False,
    )
```

profile of v0, /device:TPU:1, one launch (start us, length us, event | category | flops | bytes accessed | tf_op | source)
XLA Modules:
  0.0 359.9 jit_solution(5392411433781520436)
XLA Ops:
  11.7 3.1 fusion.27
  15.1 91.3 %all-gather.4.cloned.1.call-done = bf16[8192,768]{1,0:T(8,128)(2,1)} async-done(((bf16[256,768]{1,0:T(8,128)(2,1)}), bf16[8192,768]{1,0:T(8,128)(2,1)}) %all-gather.4.cloned.1.call-update) | async-done | bytes 12582928 | tf_op jit(solution)/shard_map/all_gather | solution.py:21
  106.4 4.8 %fusion.39 = f32[256,128]{0,1:T(8,128)S(1)} fusion(bf16[8192,768]{1,0:T(8,128)(2,1)} %all-gather.4.cloned.1.call-done, f32[128]{0:T(128)S(1)} %get-tuple-element.345, bf16[256,8192]{1,0:T(8,128)(2,1)} %param.12, f32[8192]{0:T(1024)} %param.13, f32[256]{0:T(256)S(1)} %add_rsqrt_fusion), kind=kOutput, calls=%fused_computation.45 | convolution fusion | flops 545292288 | bytes 6456832 | tf_op jit(solution)/shard_map/dot_general | solution.py:75
  111.3 3.3 fusion.45
  116.5 7.0 %fusion.36 = f32[256,512]{1,0:T(8,128)S(1)} fusion(bf16[8192,768]{1,0:T(8,128)(2,1)} %all-gather.4.cloned.1.call-done, f32[512]{0:T(512)S(1)} %convert_element_type.88, bf16[256,8192]{1,0:T(8,128)(2,1)} %param.12, f32[8192]{0:T(1024)S(1)} %copy-done.3, f32[256]{0:T(256)S(1)} %add_rsqrt_fusion), kind=kOutput, calls=%fused_computation.44 | convolution fusion | flops 2156003328 | bytes 13143040 | tf_op jit(solution)/shard_map/dot_general | solution.py:75
  124.8 59.4 %all-gather.6.cloned.1.call-done = bf16[8192,256]{0,1:T(8,128)(2,1)} async-done(((bf16[256,256]{0,1:T(8,128)(2,1)}), bf16[8192,256]{0,1:T(8,128)(2,1)}) %all-gather.6.cloned.1.call-update) | async-done | bytes 4194320 | tf_op jit(solution)/shard_map/all_gather | solution.py:21
  184.2 4.0 %fusion.57 = (bf16[8192,128]{0,1:T(8,128)(2,1)S(1)}, bf16[8192,128]{0,1:T(8,128)(2,1)}) fusion(bf16[8192,256]{0,1:T(8,128)(2,1)} %all-gather.6.cloned.1.call-done), kind=kLoop, calls=%fused_computation.81 | loop fusion | bytes 8388608 | tf_op jit(solution)/shard_map/split | solution.py:22
  188.1 61.5 %while.20 = (s32[]{:T(128)}, f32[1,4,256]{2,1,0:T(4,128)S(1)}, f32[1,4,256]{2,1,0:T(4,128)S(1)}, f32[1,4,256,128]{3,2,1,0:T(8,128)S(1)}, s32[256]{0:T(256)S(1)},...) while((s32[]{:T(128)}, f32[1,4,256]{2,1,0:T(4,128)S(1)}, ...), condition=%wide.region_9.10_spmd.clone, body=%wide.region_5.9_spmd.clone.sunk | while | flops 1103001856 | bytes 63286520 | solution.py:134
  189.7 5.8 %fusion.69 = (f32[4,256]{1,0:T(4,128)S(1)}, f32[2048,256,4]{1,0,2:T(8,128)}) fusion(pred[256,2048]{0,1:T(8,128)(4,1)S(1)} %compare_and_fusion.2, bf16[256,1,4,128]{3,0,2,1:T(8,128)(2,1)S(1)} %get-tuple-element.450, bf16[8192,128]{0,1:T(8,128)(2,1)} %get-tuple-element.449, s32[]{:T(128)S(6)} %select_n.94), kind=kOutput, calls=%fused_computation.3.clone.1 | convolution fusion | flops 543161344 | bytes 9703428 | tf_op jit(solution)/shard_map/while/body/eval_jaxpr/qkgd,nkd->kgqn/dot_general | solution.py:113
  195.5 5.3 %fusion.72 = f32[1,4,256,128]{3,2,1,0:T(8,128)S(1)} fusion(f32[2048,256,4]{1,0,2:T(8,128)} %get-tuple-element.413, f32[4,256]{1,0:T(4,128)S(1)} %bitcast.99, pred[256,2048]{0,1:T(8,128)(4,1)S(1)} %compare_and_fusion.2, f32[1,4,256,128]{3,2,1,0:T(8,128)S(1)} %get-tuple-element.432, bf16[8192,128]{0,1:T(8,128)(2,1)S(1)} %get-tuple-element.451, ...), kind=kOutput, calls=%fused_computation.11.clone.1 | convolution fusion | flops 547749888 | bytes 10493957 | tf_op jit(solution)/shard_map/while/body/eval_jaxpr/kgqn,nkd->kgqd/dot_general | solution.py:125
  201.5 2.1 fusion.71
  205.2 5.8 %fusion.69 = (f32[4,256]{1,0:T(4,128)S(1)}, f32[2048,256,4]{1,0,2:T(8,128)}) fusion(pred[256,2048]{0,1:T(8,128)(4,1)S(1)} %compare_and_fusion.2, bf16[256,1,4,128]{3,0,2,1:T(8,128)(2,1)S(1)} %get-tuple-element.450, bf16[8192,128]{0,1:T(8,128)(2,1)} %get-tuple-element.449, s32[]{:T(128)S(6)} %select_n.94), kind=kOutput, calls=%fused_computation.3.clone.1 | convolution fusion | flops 543161344 | bytes 9703428 | tf_op jit(solution)/shard_map/while/body/eval_jaxpr/qkgd,nkd->kgqn/dot_general | solution.py:113
  211.0 5.1 %fusion.72 = f32[1,4,256,128]{3,2,1,0:T(8,128)S(1)} fusion(f32[2048,256,4]{1,0,2:T(8,128)} %get-tuple-element.413, f32[4,256]{1,0:T(4,128)S(1)} %bitcast.99, pred[256,2048]{0,1:T(8,128)(4,1)S(1)} %compare_and_fusion.2, f32[1,4,256,128]{3,2,1,0:T(8,128)S(1)} %get-tuple-element.432, bf16[8192,128]{0,1:T(8,128)(2,1)S(1)} %get-tuple-element.451, ...), kind=kOutput, calls=%fused_computation.11.clone.1 | convolution fusion | flops 547749888 | bytes 10493957 | tf_op jit(solution)/shard_map/while/body/eval_jaxpr/kgqn,nkd->kgqd/dot_general | solution.py:125
  220.5 5.9 %fusion.69 = (f32[4,256]{1,0:T(4,128)S(1)}, f32[2048,256,4]{1,0,2:T(8,128)}) fusion(pred[256,2048]{0,1:T(8,128)(4,1)S(1)} %compare_and_fusion.2, bf16[256,1,4,128]{3,0,2,1:T(8,128)(2,1)S(1)} %get-tuple-element.450, bf16[8192,128]{0,1:T(8,128)(2,1)} %get-tuple-element.449, s32[]{:T(128)S(6)} %select_n.94), kind=kOutput, calls=%fused_computation.3.clone.1 | convolution fusion | flops 543161344 | bytes 9703428 | tf_op jit(solution)/shard_map/while/body/eval_jaxpr/qkgd,nkd->kgqn/dot_general | solution.py:113
  226.4 5.1 %fusion.72 = f32[1,4,256,128]{3,2,1,0:T(8,128)S(1)} fusion(f32[2048,256,4]{1,0,2:T(8,128)} %get-tuple-element.413, f32[4,256]{1,0:T(4,128)S(1)} %bitcast.99, pred[256,2048]{0,1:T(8,128)(4,1)S(1)} %compare_and_fusion.2, f32[1,4,256,128]{3,2,1,0:T(8,128)S(1)} %get-tuple-element.432, bf16[8192,128]{0,1:T(8,128)(2,1)S(1)} %get-tuple-element.451, ...), kind=kOutput, calls=%fused_computation.11.clone.1 | convolution fusion | flops 547749888 | bytes 10493957 | tf_op jit(solution)/shard_map/while/body/eval_jaxpr/kgqn,nkd->kgqd/dot_general | solution.py:125
  232.2 2.1 fusion.71
  235.9 5.8 %fusion.69 = (f32[4,256]{1,0:T(4,128)S(1)}, f32[2048,256,4]{1,0,2:T(8,128)}) fusion(pred[256,2048]{0,1:T(8,128)(4,1)S(1)} %compare_and_fusion.2, bf16[256,1,4,128]{3,0,2,1:T(8,128)(2,1)S(1)} %get-tuple-element.450, bf16[8192,128]{0,1:T(8,128)(2,1)} %get-tuple-element.449, s32[]{:T(128)S(6)} %select_n.94), kind=kOutput, calls=%fused_computation.3.clone.1 | convolution fusion | flops 543161344 | bytes 9703428 | tf_op jit(solution)/shard_map/while/body/eval_jaxpr/qkgd,nkd->kgqn/dot_general | solution.py:113
  241.7 5.1 %fusion.72 = f32[1,4,256,128]{3,2,1,0:T(8,128)S(1)} fusion(f32[2048,256,4]{1,0,2:T(8,128)} %get-tuple-element.413, f32[4,256]{1,0:T(4,128)S(1)} %bitcast.99, pred[256,2048]{0,1:T(8,128)(4,1)S(1)} %compare_and_fusion.2, f32[1,4,256,128]{3,2,1,0:T(8,128)S(1)} %get-tuple-element.432, bf16[8192,128]{0,1:T(8,128)(2,1)S(1)} %get-tuple-element.451, ...), kind=kOutput, calls=%fused_computation.11.clone.1 | convolution fusion | flops 547749888 | bytes 10493957 | tf_op jit(solution)/shard_map/while/body/eval_jaxpr/kgqn,nkd->kgqd/dot_general | solution.py:125
  247.6 2.1 fusion.71
  249.9 18.6 %all-gather.8.cloned.1.call-done = bf16[512,8192]{1,0:T(8,128)(2,1)} async-done(((bf16[512,256]{1,0:T(8,128)(2,1)}), bf16[512,8192]{1,0:T(8,128)(2,1)}) %all-gather.8.cloned.1.call-update) | async-done | bytes 8388624 | tf_op jit(solution)/shard_map/all_gather | solution.py:143
  268.6 7.7 %convolution_convert_fusion = bf16[256,8192]{1,0:T(8,128)(2,1)} fusion(bf16[256,512]{0,1:T(8,128)(2,1)S(1)} %bitcast.101, bf16[512,8192]{1,0:T(8,128)(2,1)} %all-gather.8.cloned.1.call-done), kind=kOutput, calls=%fused_computation.34 | convolution fusion | flops 2149580800 | bytes 12845056 | tf_op jit(solution)/shard_map/dot_general | solution.py:141
  276.3 47.2 %reduce-scatter.3.cloned.1.call-done = bf16[64,8192]{1,0:T(8,128)(2,1)} async-done(((bf16[256,8192]{1,0:T(8,128)(2,1)}), bf16[64,8192]{1,0:T(8,128)(2,1)}) %reduce-scatter.3.cloned.1.call-update) | async-done | bytes 1048592 | tf_op jit(solution)/shard_map/reduce_scatter | solution.py:27
  323.5 27.5 %reduce-scatter.5.cloned.1.call-done = bf16[32,8192]{1,0:T(8,128)(2,1)} async-done(((bf16[64,8192]{1,0:T(8,128)(2,1)}), bf16[32,8192]{1,0:T(8,128)(2,1)}) %reduce-scatter.5.cloned.1.call-update) | async-done | bytes 524304 | tf_op jit(solution)/shard_map/reduce_scatter | solution.py:27
  351.1 2.3 convert_add_fusion
  (85 shorter events, 20.0 us)
Async XLA Ops:
  6.5 99.9 %all-gather.4.cloned.1.call-start = ((), (), s32[]{:S(2)}) async-start(), calls=%async_computation.2 | async-start | bytes 12976128 | tf_op jit(solution)/shard_map/all_gather | solution.py:21
  6.5 104.7 %copy-start.3 = (f32[8192]{0:T(1024)S(1)}, f32[8192]{0:T(1024)}, u32[]{:S(2)}) copy-start(f32[8192]{0:T(1024)} %param.13) | copy-start | bytes 98308
  9.2 175.0 %all-gather.6.cloned.1.call-start = ((), (), s32[]{:S(2)}) async-start(), calls=%async_computation.3 | async-start | bytes 4325376 | tf_op jit(solution)/shard_map/all_gather | solution.py:21
  106.4 4.9 %copy-start.1 = (bf16[256,8192]{1,0:T(8,128)(2,1)S(1)}, bf16[256,8192]{1,0:T(8,128)(2,1)}, u32[]{:S(2)}) copy-start(bf16[256,8192]{1,0:T(8,128)(2,1)} %param.12) | copy-start | bytes 12582916
  106.4 9.9 %copy-start.2 = (bf16[512]{0:T(512)(128)(2,1)S(1)}, bf16[512]{0:T(512)(128)(2,1)}, u32[]{:S(2)}) copy-start(bf16[512]{0:T(512)(128)(2,1)} %param.17) | copy-start | bytes 3076
  106.4 9.9 %copy-start.4 = (s32[4]{0:T(128)S(1)}, s32[4]{0:T(128)}, u32[]{:S(2)}) copy-start(s32[4]{0:T(128)} %param.21) | copy-start | bytes 52
  115.3 153.2 %all-gather.8.cloned.1.call-start = ((), (), s32[]{:S(2)}) async-start(), calls=%async_computation.4 | async-start | bytes 8650752 | tf_op jit(solution)/shard_map/all_gather | solution.py:143
  116.1 207.4 %reduce-scatter.3.cloned.1.call-start = ((), (), s32[]{:S(2)}) async-start(), calls=%async_computation.5 | async-start | bytes 5242880 | tf_op jit(solution)/shard_map/reduce_scatter | solution.py:27
  195.5 6.0 %copy-start = (f32[2048,256,4]{1,0,2:T(8,128)S(1)}, f32[2048,256,4]{1,0,2:T(8,128)}, u32[]{:S(2)}) copy-start(f32[2048,256,4]{1,0,2:T(8,128)} %get-tuple-element.413) | copy-start | bytes 25165828 | tf_op jit(solution)/shard_map/while
  211.0 5.8 %copy-start = (f32[2048,256,4]{1,0,2:T(8,128)S(1)}, f32[2048,256,4]{1,0,2:T(8,128)}, u32[]{:S(2)}) copy-start(f32[2048,256,4]{1,0,2:T(8,128)} %get-tuple-element.413) | copy-start | bytes 25165828 | tf_op jit(solution)/shard_map/while
  226.4 5.8 %copy-start = (f32[2048,256,4]{1,0,2:T(8,128)S(1)}, f32[2048,256,4]{1,0,2:T(8,128)}, u32[]{:S(2)}) copy-start(f32[2048,256,4]{1,0,2:T(8,128)} %get-tuple-element.413) | copy-start | bytes 25165828 | tf_op jit(solution)/shard_map/while
  241.7 5.8 %copy-start = (f32[2048,256,4]{1,0,2:T(8,128)S(1)}, f32[2048,256,4]{1,0,2:T(8,128)}, u32[]{:S(2)}) copy-start(f32[2048,256,4]{1,0,2:T(8,128)} %get-tuple-element.413) | copy-start | bytes 25165828 | tf_op jit(solution)/shard_map/while
  276.3 74.8 %reduce-scatter.5.cloned.1.call-start = ((), (), s32[]{:S(2)}) async-start(), calls=%async_computation.6 | async-start | bytes 1572864 | tf_op jit(solution)/shard_map/reduce_scatter | solution.py:27
Sparse Core Ops, SparseCore 0:
  9.9 96.5 all-gather.3
  115.4 68.6 all-gather.5
  186.6 81.8 all-gather.7
  276.4 47.0 reduce-scatter.2
  325.9 25.1 reduce-scatter.4
where the time goes:
time: 360 us
  waiting for transfers between devices  245 us (68%)
  matrix products  66.7 us (19%)
  other arithmetic  25.7 us (7%)
  between operations  13.3 us (4%)
  local copies, waits for them, and re-layouts  8.8 us (2%)
    all_gather x2, waiting for transfers between devices, side_by_side(): filled = lax.all_gather(both, axis, axis=dim, tiled=True)  151 us
    reduce_scatter x2, waiting for transfers between devices, scatter_axes(): array = lax.psum_scatter(array, axis, scatter_dimension=dim, tiled=True)  74.7 us
    dot_general x4, matrix products, fold_block(): jnp.einsum('qkgd,nkd->kgqn', query_grid, key_block, preferred_element_typ...  23.2 us
    dot_general x4, matrix products, fold_block(): jnp.einsum('kgqn,nkd->kgqd', weights.astype(jnp.bfloat16), value_block, p...  20.7 us
    all_gather x1, waiting for transfers between devices, shards(): lax.all_gather(w_out, 'fsdp', axis=1, tiled=True)  18.6 us
    dot_general x3, matrix products, shards(): jnp.dot(normed, piece, preferred_element_type=jnp.float32)  15.1 us
    reduce_sum x4, other arithmetic, fold_block(): total = total * factor + jnp.sum(weights, axis=3)  8.28 us
    dot_general x1, matrix products, shards(): jnp.dot(attended, lax.all_gather(w_out, 'fsdp', axis=1, tiled=True), pref...  7.69 us
  transfers between devices with their start and end apart: 5, of which 5 were waited for; matrix products, arithmetic and copies ran while one was open for 21% of the time, Pallas kernels for 0%

commit v1 on v0

--- a/solution.py
+++ b/solution.py
@@ -140,7 +140,9 @@
     ).astype(jnp.float32)
     terms = jnp.dot(
         attended,
-        lax.all_gather(w_out, "fsdp", axis=1, tiled=True),
+        jnp.concatenate(
+            lax.all_to_all(jnp.stack([w_out] * lax.axis_size("fsdp")), "fsdp", 0, 0), axis=1
+        ),
         preferred_element_type=jnp.float32,
     )
     summed = scatter_axes(terms.astype(jnp.bfloat16), TP, 0).astype(jnp.float32)

time: 360 us -> 471 us (1.31)
  waiting for transfers between devices: 245 us -> 363 us
  matrix products: 66.7 us -> 43.9 us
  starting transfers between devices: 0.35 us -> 13.4 us
    all_gather x2, waiting for transfers between devices: 151 us -> 255 us  [side_by_side(): filled = lax.all_gather(both, axis, axis=dim, tiled=True)]
    reduce_scatter x2, waiting for transfers between devices: 74.7 us -> 108 us  [scatter_axes(): array = lax.psum_scatter(array, axis, scatter_dimension=dim, tiled=True)]
    all_gather x1 -> x0, waiting for transfers between devices: 18.6 us -> none  [shards(): lax.all_gather(w_out, 'fsdp', axis=1, tiled=True)]
    all_to_all x0 -> x1, starting transfers between devices: none -> 13.3 us  [shards(): lax.all_to_all(jnp.stack([w_out] * lax.axis_size('fsdp')), 'fsdp', 0, 0)]
    dot_general x4, matrix products: 23.2 us -> 10.3 us  [fold_block(): jnp.einsum('qkgd,nkd->kgqn', query_grid, key_block, preferred_element_typ...]
    dot_general x4, matrix products: 20.7 us -> 10.7 us  [fold_block(): jnp.einsum('kgqn,nkd->kgqd', weights.astype(jnp.bfloat16), value_block, p...]
  transfers between devices with their start and end apart: 5 -> 5, of which waited for: 5 -> 4; matrix products, arithmetic and copies ran while one was open for 21% -> 12% of each run, Pallas kernels for 0% -> 0%
where the time goes in v1:
time: 471 us; the launch traced here: 470 us
  waiting for transfers between devices  363 us (77%)
  matrix products  43.9 us (9%)
  other arithmetic  25.8 us (5%)
  starting transfers between devices  13.4 us (3%)
  between operations  13.4 us (3%)
  local copies, waits for them, and re-layouts  10.3 us (2%)
    all_gather x2, waiting for transfers between devices, side_by_side(): filled = lax.all_gather(both, axis, axis=dim, tiled=True)  255 us
    reduce_scatter x2, waiting for transfers between devices, scatter_axes(): array = lax.psum_scatter(array, axis, scatter_dimension=dim, tiled=True)  108 us
    dot_general x3, matrix products, shards(): jnp.dot(normed, piece, preferred_element_type=jnp.float32)  15.2 us
    all_to_all x1, starting transfers between devices, shards(): lax.all_to_all(jnp.stack([w_out] * lax.axis_size('fsdp')), 'fsdp', 0, 0)  13.3 us
    dot_general x4, matrix products, fold_block(): jnp.einsum('kgqn,nkd->kgqd', weights.astype(jnp.bfloat16), value_block, p...  10.7 us
    dot_general x4, matrix products, fold_block(): jnp.einsum('qkgd,nkd->kgqn', query_grid, key_block, preferred_element_typ...  10.3 us
  transfers between devices with their start and end apart: 5, of which 4 were waited for; matrix products, arithmetic and copies ran while one was open for 12% of the time, Pallas kernels for 0%

profile of v1, /device:TPU:1, one launch (start us, length us, event | category | flops | bytes accessed | tf_op | source)
XLA Modules:
  0.0 470.1 jit_solution(3223049314585627442)
XLA Ops:
  11.7 3.1 fusion.27
  15.1 91.3 %all-gather.3.cloned.1.call-done = bf16[8192,768]{1,0:T(8,128)(2,1)} async-done(((bf16[256,768]{1,0:T(8,128)(2,1)}), bf16[8192,768]{1,0:T(8,128)(2,1)}) %all-gather.3.cloned.1.call-update) | async-done | bytes 12582928 | tf_op jit(solution)/shard_map/all_gather | solution.py:21
  106.4 4.8 %fusion.39 = f32[256,128]{0,1:T(8,128)S(1)} fusion(bf16[8192,768]{1,0:T(8,128)(2,1)} %all-gather.3.cloned.1.call-done, f32[128]{0:T(128)S(1)} %get-tuple-element.345, bf16[256,8192]{1,0:T(8,128)(2,1)} %param.12, f32[8192]{0:T(1024)} %param.13, f32[256]{0:T(256)S(1)} %add_rsqrt_fusion), kind=kOutput, calls=%fused_computation.45 | convolution fusion | flops 545292288 | bytes 6456832 | tf_op jit(solution)/shard_map/dot_general | solution.py:75
  111.3 3.3 fusion.45
  115.5 4.2 stack.2
  119.7 13.3 %all-to-all-start = ((bf16[32,512,256]{1,2,0:T(8,128)(2,1)}), bf16[32,512,256]{1,2,0:T(8,128)(2,1)}, u32[]{:S(2)}, u32[]{:S(2)}) async-start(bf16[32,512,256]{1,2,0:T(8,128)(2,1)} %stack.2), calls=%async_computation | async-start | bytes 16777216 | tf_op jit(solution)/shard_map/all_to_all | solution.py:144
  133.3 7.1 %fusion.36 = f32[256,512]{1,0:T(8,128)S(1)} fusion(bf16[8192,768]{1,0:T(8,128)(2,1)} %all-gather.3.cloned.1.call-done, f32[512]{0:T(512)S(1)} %convert_element_type.88, bf16[256,8192]{1,0:T(8,128)(2,1)} %param.12, f32[8192]{0:T(1024)S(1)} %copy-done.3, f32[256]{0:T(256)S(1)} %add_rsqrt_fusion), kind=kOutput, calls=%fused_computation.44 | convolution fusion | flops 2156003328 | bytes 13143040 | tf_op jit(solution)/shard_map/dot_general | solution.py:75
  141.6 163.4 %all-gather.5.cloned.1.call-done = bf16[8192,256]{0,1:T(8,128)(2,1)} async-done(((bf16[256,256]{0,1:T(8,128)(2,1)}), bf16[8192,256]{0,1:T(8,128)(2,1)}) %all-gather.5.cloned.1.call-update) | async-done | bytes 4194320 | tf_op jit(solution)/shard_map/all_gather | solution.py:21
  305.0 3.9 fusion.57
  308.9 35.9 %while.20 = (s32[]{:T(128)}, f32[1,4,256]{2,1,0:T(4,128)S(1)}, f32[1,4,256]{2,1,0:T(4,128)S(1)}, f32[1,4,256,128]{3,2,1,0:T(8,128)S(1)}, s32[256]{0:T(256)S(1)},...) while((s32[]{:T(128)}, f32[1,4,256]{2,1,0:T(4,128)S(1)}, ...), condition=%wide.region_9.10_spmd.clone, body=%wide.region_5.9_spmd.clone.sunk | while | flops 1103001856 | bytes 29732068 | solution.py:134
  310.5 2.6 fusion.69
  313.1 2.1 fusion.71
  315.2 2.7 fusion.72
  319.5 2.6 fusion.69
  324.2 2.7 fusion.72
  328.5 2.6 fusion.69
  333.2 2.7 fusion.72
  337.5 2.6 fusion.69
  340.1 2.1 fusion.71
  342.2 2.7 fusion.72
  345.2 7.7 %convolution_convert_fusion = bf16[256,8192]{1,0:T(8,128)(2,1)} fusion(bf16[256,512]{0,1:T(8,128)(2,1)S(1)} %bitcast.105, bf16[512,8192]{0,1:T(8,128)(2,1)} %bitcast.12), kind=kOutput, calls=%fused_computation.34 | convolution fusion | flops 2149580800 | bytes 12845056 | tf_op jit(solution)/shard_map/dot_general | solution.py:141
  353.0 80.8 %reduce-scatter.3.cloned.1.call-done = bf16[64,8192]{1,0:T(8,128)(2,1)} async-done(((bf16[256,8192]{1,0:T(8,128)(2,1)}), bf16[64,8192]{1,0:T(8,128)(2,1)}) %reduce-scatter.3.cloned.1.call-update) | async-done | bytes 1048592 | tf_op jit(solution)/shard_map/reduce_scatter | solution.py:27
  433.7 27.5 %reduce-scatter.5.cloned.1.call-done = bf16[32,8192]{1,0:T(8,128)(2,1)} async-done(((bf16[64,8192]{1,0:T(8,128)(2,1)}), bf16[32,8192]{1,0:T(8,128)(2,1)}) %reduce-scatter.5.cloned.1.call-update) | async-done | bytes 524304 | tf_op jit(solution)/shard_map/reduce_scatter | solution.py:27
  461.3 2.3 convert_add_fusion
  (80 shorter events, 18.6 us)
Async XLA Ops:
  6.5 99.9 %all-gather.3.cloned.1.call-start = ((), (), s32[]{:S(2)}) async-start(), calls=%async_computation.3 | async-start | bytes 12976128 | tf_op jit(solution)/shard_map/all_gather | solution.py:21
  6.5 104.7 %copy-start.3 = (f32[8192]{0:T(1024)S(1)}, f32[8192]{0:T(1024)}, u32[]{:S(2)}) copy-start(f32[8192]{0:T(1024)} %param.13) | copy-start | bytes 98308
  9.2 295.8 %all-gather.5.cloned.1.call-start = ((), (), s32[]{:S(2)}) async-start(), calls=%async_computation.4 | async-start | bytes 4325376 | tf_op jit(solution)/shard_map/all_gather | solution.py:21
  106.4 4.9 %copy-start = (bf16[256,8192]{1,0:T(8,128)(2,1)S(1)}, bf16[256,8192]{1,0:T(8,128)(2,1)}, u32[]{:S(2)}) copy-start(bf16[256,8192]{1,0:T(8,128)(2,1)} %param.12) | copy-start | bytes 12582916
  106.4 8.9 %copy-start.1 = (bf16[512,256]{1,0:T(8,128)(2,1)S(1)}, bf16[512,256]{1,0:T(8,128)(2,1)}, u32[]{:S(2)}) copy-start(bf16[512,256]{1,0:T(8,128)(2,1)} %param.20) | copy-start | bytes 786436
  119.7 13.4 %copy-start.4 = (s32[4]{0:T(128)S(1)}, s32[4]{0:T(128)}, u32[]{:S(2)}) copy-start(s32[4]{0:T(128)} %param.21) | copy-start | bytes 52
  119.7 13.5 %copy-start.2 = (bf16[512]{0:T(512)(128)(2,1)S(1)}, bf16[512]{0:T(512)(128)(2,1)}, u32[]{:S(2)}) copy-start(bf16[512]{0:T(512)(128)(2,1)} %param.17) | copy-start | bytes 3076
  119.7 225.4 %all-to-all-start = ((bf16[32,512,256]{1,2,0:T(8,128)(2,1)}), bf16[32,512,256]{1,2,0:T(8,128)(2,1)}, u32[]{:S(2)}, u32[]{:S(2)}) async-start(bf16[32,512,256]{1,2,0:T(8,128)(2,1)} %stack.2), calls=%async_computation | async-start | bytes 16777216 | tf_op jit(solution)/shard_map/all_to_all | solution.py:144
  133.0 300.7 %reduce-scatter.3.cloned.1.call-start = ((), (), s32[]{:S(2)}) async-start(), calls=%async_computation.5 | async-start | bytes 5242880 | tf_op jit(solution)/shard_map/reduce_scatter | solution.py:27
  352.9 108.4 %reduce-scatter.5.cloned.1.call-start = ((), (), s32[]{:S(2)}) async-start(), calls=%async_computation.6 | async-start | bytes 1572864 | tf_op jit(solution)/shard_map/reduce_scatter | solution.py:27
Sparse Core Ops, SparseCore 0:
  9.9 96.5 all-gather.2
  115.5 189.5 all-gather.4
  353.0 80.6 reduce-scatter.2
  436.1 25.1 reduce-scatter.4
